TPU v7x, 32 devices: a whole 2x2x4 slice. The times are simulated.
32 devices in a mesh: section: 1, grp: 16 (over z, x, core), tp: 2 (over y).
Axes of the slice: x: 2, y: 2, z: 4, core: 2. Of those that a mesh axis runs over, the one named last changes fastest.
Arguments:
- partials: bfloat16 [2, 1, 2048, 8192], P('tp', 'section', 'grp'), may hold values from -3 to 3
- residual: bfloat16 [1, 2048, 8192], P('section', 'grp', 'tp'), may hold values from -300 to 300
- norm_gain: bfloat16 [8192], replicated, may hold values from 0.099609375 to 1.8984375
- w_query: bfloat16 [8192, 8192], P('grp', ('section', 'tp')), may hold values from -0.0625 to 0.0625
- w_keyval: bfloat16 [8192, 2048], P('grp', ('section', 'tp')), may hold values from -0.0625 to 0.0625
- bias_query: bfloat16 [8192], P(('section', 'tp')), may hold values from -3 to 3
- bias_keyval: bfloat16 [2048], P(('section', 'tp')), may hold values from -3 to 3
Outputs:
- hidden: bfloat16 [1, 2048, 8192], P('section', 'grp', 'tp')
- query: bfloat16 [1, 2048, 8192], P(None, 'grp', ('section', 'tp'))
- keyval: bfloat16 [1, 2048, 2048], P(None, 'grp', ('section', 'tp'))
All inputs are finite; a program needn't handle non-finite values.
Results may differ from a plain program's by a relative error of at most 0.01.
Values may be sent and summed in bfloat16 or wider, within the bound.
A program may use at most 192 MiB of HBM per device.

v0:
```python
import functools
import math

import jax
import jax.numpy as jnp
from jax import lax
from jax.experimental import pallas as pl
from jax.experimental.pallas import tpu as pltpu
from jax.sharding import PartitionSpec as P

epsilon = 1e-06
MESH = pl.DeviceIdType.MESH
CORES = 2
SIDES = 2


def kernel(ranks, parts, width, rows_ref, wq_ref, wk_ref, square_ref, bias_ref,
           query_ref, keyval_ref, xs, wide, side_out, side_in, rank_out, rank_in, own, squares,
           w_local, w_send, w_recv, x_local, x_send, x_recv, f_send, f_recv, q_send, q_recv,
           s_send, s_recv, r_send, r_recv):
    me = lax.axis_index("grp")
    part = lax.axis_index("tp")
    core = lax.rem(me, CORES)
    chip = me // CORES
    side = lax.rem(chip, SIDES)
    rank = chip // SIDES
    chips = ranks * SIDES
    mate = chip * CORES + (1 - core)
    depth, q_cols = wq_ref.shape
    k_cols = wk_ref.shape[1]
    share = CORES * depth
    steps = (q_cols + k_cols) // width

    def device(at_rank, at_side):
        return (at_rank * SIDES + at_side) * CORES + core

    barrier = pltpu.get_barrier_semaphore()
    pl.semaphore_signal(barrier, inc=1, device_id={"grp": mate}, device_id_type=MESH)
    for d in range(parts):
        for off in range(chips):
            if d or off:
                to = lax.rem(chip + off, chips) * CORES + core
                pl.semaphore_signal(
                    barrier, inc=1, device_id={"grp": to, "tp": lax.rem(part + d, parts)},
                    device_id_type=MESH)
    pl.semaphore_wait(barrier, chips * parts)

    held = chips // parts
    piece = rows_ref.shape[0] // parts
    whole_here = chip // held == part

    def piece_of(index):
        return pl.ds(pl.multiple_of(index * piece, piece), piece)

    def x_ends(i, d):
        rows = piece_of(lax.rem(part + d, parts))
        return rows_ref.at[rows, pl.ds(i * share, share)], xs.at[chip, rows]

    def x_copy(i, d):
        src, dst = x_ends(i, d)
        return pltpu.make_async_remote_copy(
            src_ref=src, dst_ref=dst, send_sem=x_send.at[i, d], recv_sem=x_recv.at[chip],
            device_id={"grp": (part * held + i) * CORES + core, "tp": lax.rem(part + d, parts)},
            device_id_type=MESH)

    def x_own(i):
        src, dst = x_ends(i, 0)
        return pltpu.make_async_copy(src, dst, x_local)

    def each_x(far, near):
        for i in range(held):
            here = jnp.logical_and(whole_here, lax.rem(chip, held) == i)
            pl.when(here)(functools.partial(near, i))
            pl.when(jnp.logical_not(here))(functools.partial(far, i, 0))
            for d in range(1, parts):
                far(i, d)

    each_x(lambda i, d: x_copy(i, d).start(), lambda i: x_own(i).start())

    def q_copy(d):
        return pltpu.make_async_remote_copy(
            src_ref=square_ref, dst_ref=squares.at[d],
            send_sem=q_send.at[d], recv_sem=q_recv.at[d],
            device_id={"tp": lax.rem(part + d, parts)}, device_id_type=MESH)

    for d in range(1, parts):
        q_copy(d).start()

    def x_arrive(source):
        pltpu.make_async_remote_copy(
            src_ref=xs.at[source, piece_of(part)], dst_ref=xs.at[source, piece_of(part)],
            send_sem=x_send.at[0, 0], recv_sem=x_recv.at[source],
            device_id={"grp": mate}, device_id_type=MESH).wait_recv()

    def f_copy(source, d):
        return pltpu.make_async_remote_copy(
            src_ref=xs.at[source, piece_of(part)], dst_ref=xs.at[source, piece_of(part)],
            send_sem=f_send.at[source, d], recv_sem=f_recv.at[source, d],
            device_id={"tp": lax.rem(part + d, parts)}, device_id_type=MESH)

    def pass_on(source, here):
        if here:
            def near():
                for i in range(held):
                    pl.when(lax.rem(chip, held) == i)(lambda i=i: x_own(i).wait())

            pl.when(whole_here)(near)
            pl.when(jnp.logical_not(whole_here))(lambda: x_arrive(source))
        else:
            x_arrive(source)
        for d in range(1, parts):
            f_copy(source, d).start()

    def x_wait(source):
        for d in range(1, parts):
            rows = piece_of(lax.rem(part + parts - d, parts))
            pltpu.make_async_remote_copy(
                src_ref=xs.at[source, rows], dst_ref=xs.at[source, rows],
                send_sem=f_send.at[source, d], recv_sem=f_recv.at[source, d],
                device_id={"grp": mate}, device_id_type=MESH).wait_recv()

    mine = pl.ds(pl.multiple_of(core * depth, depth), depth)
    q_part = wide.at[mine, pl.ds(0, q_cols)]
    k_part = wide.at[mine, pl.ds(q_cols, k_cols)]
    locals_ = [pltpu.make_async_copy(wq_ref, q_part, w_local.at[0]),
               pltpu.make_async_copy(wk_ref, k_part, w_local.at[1])]
    sends = [pltpu.make_async_remote_copy(
        src_ref=src, dst_ref=dst, send_sem=w_send.at[i], recv_sem=w_recv.at[i],
        device_id={"grp": mate}, device_id_type=MESH)
        for i, (src, dst) in enumerate(((wq_ref, q_part), (wk_ref, k_part)))]
    for copy in sends + locals_:
        copy.start()
    for copy in locals_:
        copy.wait()
    theirs = pl.ds(pl.multiple_of((1 - core) * depth, depth), depth)
    for i, (src, dst) in enumerate(((wq_ref, wide.at[theirs, pl.ds(0, q_cols)]),
                                    (wk_ref, wide.at[theirs, pl.ds(q_cols, k_cols)]))):
        pltpu.make_async_remote_copy(
            src_ref=src, dst_ref=dst, send_sem=w_send.at[i], recv_sem=w_recv.at[i],
            device_id={"grp": mate}, device_id_type=MESH).wait_recv()

    def columns(j):
        return pl.ds(pl.multiple_of(j * width, width), width)

    def s_copy(k, j):
        return pltpu.make_async_remote_copy(
            src_ref=side_out.at[k, :, columns(j)], dst_ref=side_in.at[k, :, columns(j)],
            send_sem=s_send.at[k, j], recv_sem=s_recv.at[k, j],
            device_id={"grp": device(rank, 1 - side)}, device_id_type=MESH)

    def r_copy(k, j):
        return pltpu.make_async_remote_copy(
            src_ref=rank_out.at[k, :, columns(j)], dst_ref=rank_in.at[k, :, columns(j)],
            send_sem=r_send.at[k, j], recv_sem=r_recv.at[k, j],
            device_id={"grp": device(lax.rem(rank + k, ranks), side)}, device_id_type=MESH)

    order = list(range(1, ranks)) + [0]
    for k in order:
        source = lax.rem(rank + k, ranks) * SIDES + (1 - side)
        pass_on(source, False)
        pass_on(lax.rem(rank + k, ranks) * SIDES + side, k == 0)
        x_wait(source)

        def body(j, carry, k=k, source=source):
            side_out[k, :, columns(j)] = jnp.dot(
                xs[source], wide[:, columns(j)], preferred_element_type=jnp.float32
            ).astype(jnp.bfloat16)
            s_copy(k, j).start()
            return carry

        lax.fori_loop(0, steps, body, 0)
    for k in order:
        source = lax.rem(rank + k, ranks) * SIDES + side
        x_wait(source)

        def body(j, carry, k=k, source=source):
            total = jnp.dot(xs[source], wide[:, columns(j)], preferred_element_type=jnp.float32)
            s_copy(k, j).wait_recv()
            total = total + side_in[k, :, columns(j)].astype(jnp.float32)
            if k:
                rank_out[k, :, columns(j)] = total.astype(jnp.bfloat16)
                r_copy(k, j).start()
            else:
                own[:, columns(j)] = total
            return carry

        lax.fori_loop(0, steps, body, 0)

    mean_square = square_ref[...]
    for d in range(1, parts):
        q_copy(d).wait_recv()
        mean_square = mean_square + squares[d]
    model_width = rows_ref.shape[1] * parts
    scale = lax.rsqrt(mean_square[:, :1] / model_width + epsilon)

    def finish(first, count, out_ref):
        def body(i, carry):
            j = first + i
            total = own[:, columns(j)]
            for k in range(1, ranks):
                r_copy(k, j).wait_recv()
                total = total + rank_in[k, :, columns(j)].astype(jnp.float32)
            total = total * scale + bias_ref[:, columns(j)]
            out_ref[:, columns(i)] = total.astype(jnp.bfloat16)
            return carry

        lax.fori_loop(0, count, body, 0)

    finish(0, q_cols // width, query_ref)
    finish(q_cols // width, k_cols // width, keyval_ref)

    for copy in sends:
        copy.wait_send()
    each_x(lambda i, d: x_copy(i, d).wait_send(), lambda i: None)
    for d in range(1, parts):
        q_copy(d).wait_send()
        for source in range(chips):
            f_copy(source, d).wait_send()

    def drain(j, carry):
        for k in range(ranks):
            s_copy(k, j).wait_send()
            if k:
                r_copy(k, j).wait_send()
        return carry

    lax.fori_loop(0, steps, drain, 0)


def project(rows, w_query, w_keyval, squares, bias, group, parts):
    count = rows.shape[0]
    depth, q_cols = w_query.shape
    k_cols = w_keyval.shape[1]
    total = q_cols + k_cols
    width = math.gcd(math.gcd(q_cols, k_cols), 512)
    steps = total // width
    ranks = group // (CORES * SIDES)
    chips = group // CORES
    share = CORES * depth
    vmem = pl.BlockSpec(memory_space=pltpu.VMEM)
    hbm = pl.BlockSpec(memory_space=pl.ANY)
    dma = pltpu.SemaphoreType.DMA
    return pl.pallas_call(
        functools.partial(kernel, ranks, parts, width),
        out_shape=(jax.ShapeDtypeStruct((count, q_cols), jnp.bfloat16),
                   jax.ShapeDtypeStruct((count, k_cols), jnp.bfloat16)),
        in_specs=[vmem, hbm, hbm, vmem, vmem],
        out_specs=(vmem, vmem),
        scratch_shapes=[
            pltpu.VMEM((chips, count, share), jnp.bfloat16),
            pltpu.VMEM((share, total), jnp.bfloat16),
            pltpu.VMEM((ranks, count, total), jnp.bfloat16),
            pltpu.VMEM((ranks, count, total), jnp.bfloat16),
            pltpu.VMEM((ranks, count, total), jnp.bfloat16),
            pltpu.VMEM((ranks, count, total), jnp.bfloat16),
            pltpu.VMEM((count, total), jnp.float32),
            pltpu.VMEM((parts, count, squares.shape[1]), jnp.float32),
            dma((2,)), dma((2,)), dma((2,)),
            dma, dma((chips // parts, parts)), dma((chips,)),
            dma((chips, parts)), dma((chips, parts)), dma((parts,)), dma((parts,)),
            dma((ranks, steps)), dma((ranks, steps)),
            dma((ranks, steps)), dma((ranks, steps)),
        ],
        compiler_params=pltpu.CompilerParams(
            collective_id=0, has_side_effects=True, vmem_limit_bytes=60 * 1024 * 1024),
    )(rows, w_query, w_keyval, squares, bias)


def own_sum(partial, feature_share, parts):
    if parts != 2:
        return lax.psum_scatter(
            partial, "tp", scatter_dimension=2, tiled=True).astype(jnp.float32)
    part = lax.axis_index("tp")
    own = lax.dynamic_slice_in_dim(partial, part * feature_share, feature_share, 2)
    other = lax.dynamic_slice_in_dim(partial, (1 - part) * feature_share, feature_share, 2)
    other = lax.ppermute(other, "tp", [(0, 1), (1, 0)])
    return own.astype(jnp.float32) + other.astype(jnp.float32)


def local(group, parts, partials, residual, norm_gain, w_query, w_keyval, bias_query, bias_keyval):
    feature_share = residual.shape[2]
    summed = own_sum(partials[0], feature_share, parts)
    hidden = (residual.astype(jnp.float32) + summed).astype(jnp.bfloat16)
    widened = hidden.astype(jnp.float32)
    squares = jnp.sum(widened * widened, axis=-1)
    offset = lax.axis_index("tp") * feature_share
    local_gain = lax.dynamic_slice_in_dim(norm_gain, offset, feature_share, 0).astype(jnp.float32)
    scaled = (widened * local_gain).astype(jnp.bfloat16)
    scaled = lax.all_gather(scaled, "section", axis=0, tiled=True)
    squares = lax.all_gather(squares, "section", axis=0, tiled=True)
    seqs, length = squares.shape
    squares = jnp.broadcast_to(squares.reshape(-1, 1), (seqs * length, 128))
    bias = jnp.concatenate([bias_query, bias_keyval]).astype(jnp.float32)[None]
    query, keyval = project(
        scaled.reshape(seqs * length, feature_share), w_query, w_keyval, squares, bias,
        group, parts)
    return (hidden, query.reshape(seqs, length, -1), keyval.reshape(seqs, length, -1))


def solution(mesh):
    placed = (
        P("tp", "section", "grp", None),
        P("section", "grp", "tp"),
        P(),
        P("grp", ("section", "tp")),
        P("grp", ("section", "tp")),
        P(("section", "tp")),
        P(("section", "tp")),
    )
    return jax.shard_map(
        functools.partial(local, mesh.shape["grp"], mesh.shape["tp"]),
        mesh=mesh,
        in_specs=placed,
        out_specs=(
            P("section", "grp", "tp"),
            P(None, "grp", ("section", "tp")),
            P(None, "grp", ("section", "tp")),
        ),
        check_vma=False,
    )
```

profile of v0, /device:TPU:26, one launch (start us, length us, event | category | flops | bytes accessed | tf_op | source)
XLA Modules:
  0.0 232.8 jit_solution(2916359718282102550)
XLA Ops:
  0.6 0.0 copy-start.1
  0.6 0.0 copy-start.5
  0.7 0.0 copy-start.3
  0.7 0.0 copy-start.4
  0.7 1.4 dynamic-slice_bitcast_fusion
  2.1 1.6 collective-permute-start
  3.7 0.0 copy-done.5
  3.7 0.0 copy-done.3
  3.7 0.0 copy-done.4
  3.8 0.6 maximum_convert_fusion.bias_ref
  4.4 22.8 %collective-permute-done = bf16[1,128,4096]{2,1,0:T(8,128)(2,1)} collective-permute-done((bf16[1,128,4096]{2,1,0:T(8,128)(2,1)S(1)}, bf16[1,128,4096]{2,1,0:T(8,128)(2,1)}, u32[]{:S(2)}, u32[]{:S(2)}) %collective-permute-start) | collective-permute-done | bytes 1048608 | tf_op jit(solution)/shard_map/ppermute | solution.py:276
  27.2 0.0 copy-done.1
  27.2 2.1 fusion.1
  29.3 0.0 copy-start
  29.3 1.3 fusion.4.rows_ref
  30.6 0.7 broadcast_in_dim.2.square_ref
  31.4 198.4 %shard_map.94 = (bf16[128,4096]{1,0:T(8,128)(2,1)}, bf16[128,1024]{1,0:T(8,128)(2,1)}) custom-call(bf16[128,4096]{1,0:T(8,128)(2,1)} %fusion.4.rows_ref, bf16[512,4096]{1,0:T(8,128)(2,1)} %wq_ref.1, bf16[512,1024]{1,0:T(8,128)(2,1)} %wk_ref.1, f32[128,128]{1,0:T(8,128)} %broadcast_in_dim.2.square_ref, f32[1,5120]{1,0:T(1,128)} %maximum_convert_fusion.bias_ref), custom_call_target="tpu_custom_call" | custom-call | tf_op jit(solution)/shard_map/pallas_call | solution.py:243
  229.8 0.0 copy-done
  229.8 0.0 copy-start.2
  229.8 2.3 %copy.12 = bf16[1,128,4096]{2,1,0:T(8,128)(2,1)} copy(bf16[1,128,4096]{2,1,0:T(8,128)(2,1)} %bitcast.10) | data formatting | bytes 2097152
  232.1 0.0 copy-done.2
  232.1 0.7 copy.13
  (3 shorter events, 0.0 us)
Async XLA Ops:
  0.6 26.6 %copy-start.1 = (bf16[1,1,128,8192]{3,2,1,0:T(8,128)(2,1)S(1)}, bf16[1,1,128,8192]{3,2,1,0:T(8,128)(2,1)}, u32[]{:S(2)}) copy-start(bf16[1,1,128,8192]{3,2,1,0:T(8,128)(2,1)} %param.7) | copy-start | bytes 6291460
  0.6 3.1 %copy-start.5 = (bf16[1024]{0:T(1024)(128)(2,1)S(1)}, bf16[1024]{0:T(1024)(128)(2,1)}, u32[]{:S(2)}) copy-start(bf16[1024]{0:T(1024)(128)(2,1)} %param.13) | copy-start | bytes 6148
  0.7 3.1 %copy-start.3 = (bf16[4096]{0:T(1024)(128)(2,1)S(1)}, bf16[4096]{0:T(1024)(128)(2,1)}, u32[]{:S(2)}) copy-start(bf16[4096]{0:T(1024)(128)(2,1)} %param.12) | copy-start | bytes 24580
  0.7 3.1 %copy-start.4 = (bf16[8192]{0:T(1024)(128)(2,1)S(1)}, bf16[8192]{0:T(1024)(128)(2,1)}, u32[]{:S(2)}) copy-start(bf16[8192]{0:T(1024)(128)(2,1)} %param.9) | copy-start | bytes 49156
  2.1 25.1 %collective-permute-start = (bf16[1,128,4096]{2,1,0:T(8,128)(2,1)S(1)}, bf16[1,128,4096]{2,1,0:T(8,128)(2,1)}, u32[]{:S(2)}, u32[]{:S(2)}) collective-permute-start(bf16[1,128,4096]{2,1,0:T(8,128)(2,1)S(1)} %dynamic-slice_bitcast_fusion), channel_id=1, source_target_pairs={{0,1},{1,0},{2,3},{3,2},{4,5},{5,4},{6,7},{7,6},{8,9},{9,8},{10,11... | collective-permute-start | bytes 3145736 | tf_op jit(solution)/shard_map/ppermute | solution.py:276
  29.3 200.4 %copy-start = (bf16[1,128,4096]{2,1,0:T(8,128)(2,1)}, bf16[1,128,4096]{2,1,0:T(8,128)(2,1)S(1)}, u32[]{:S(2)}) copy-start(bf16[1,128,4096]{2,1,0:T(8,128)(2,1)S(1)} %get-tuple-element.12) | copy-start | bytes 3145732
  229.8 2.3 %copy-start.2 = (bf16[128,1024]{1,0:T(8,128)(2,1)S(1)}, bf16[128,1024]{1,0:T(8,128)(2,1)}, u32[]{:S(2)}) copy-start(bf16[128,1024]{1,0:T(8,128)(2,1)} %get-tuple-element.6) | copy-start | bytes 786436
where the time goes:
time: 233 us
  Pallas kernels  198 us (85%)
  waiting for transfers between devices  22.8 us (10%)
  local copies, waits for them, and re-layouts  5.23 us (2%)
  other arithmetic  4.08 us (2%)
    pallas_call x1, Pallas kernels, project(): pl.pallas_call(functools.partial(kernel, ranks, parts, width), out_shape=...  198 us
    ppermute x1, waiting for transfers between devices, own_sum(): other = lax.ppermute(other, 'tp', [(0, 1), (1, 0)])  22.8 us
  transfers between devices with their start and end apart: 1, of which 1 were waited for; matrix products, arithmetic and copies ran while one was open for 0% of the time, Pallas kernels for 0%

commit v1 on v0

v1 whole, which is shorter than its diff:
```python
import functools
import math

import jax
import jax.numpy as jnp
from jax import lax
from jax.experimental import pallas as pl
from jax.experimental.pallas import tpu as pltpu
from jax.sharding import PartitionSpec as P

epsilon = 1e-06
MESH = pl.DeviceIdType.MESH
CORES = 2
SIDES = 2
LAG = 2


def kernel(ranks, parts, chunks, width, early, fused, *refs):
    refs = list(refs)
    take = lambda n: [refs.pop(0) for _ in range(n)]
    if fused:
        partial_ref, residual_ref, gain_ref = take(3)
    else:
        given_rows, given_squares = take(2)
    wq_ref, wk_ref, bias_ref = take(3)
    if fused:
        hidden_ref, = take(1)
    query_ref, keyval_ref = take(2)
    if fused:
        own_part, own_residual, part_in, rows_ref, square_ref = take(5)
        h_local, p_send, p_recv = take(3)
    else:
        rows_ref, square_ref = given_rows, given_squares
    (xs, wide, products, right_out, right_in, left_out, left_in, squares, scale_ref,
     w_local, m_send, m_recv, wx_send, wx_recv, wf_send, wf_recv,
     x_send, x_recv, f_send, f_recv, q_send, q_recv,
     rt_send, rt_recv, lt_send, lt_recv) = refs

    me = lax.axis_index("grp")
    part = lax.axis_index("tp")
    core = lax.rem(me, CORES)
    chip = me // CORES
    side = lax.rem(chip, SIDES)
    rank = chip // SIDES
    depth, q_cols = wq_ref.shape
    k_cols = wk_ref.shape[1]
    share = SIDES * CORES * depth
    q_steps = q_cols // width
    columns_count = (q_cols + k_cols) // width
    count, feature_share = rows_ref.shape
    rows = count // chunks
    piece = rows // parts
    held = ranks // parts
    steps = chunks * columns_count
    slots = products.shape[0]

    def grp(at_rank, at_side, at_core):
        return (at_rank * SIDES + at_side) * CORES + at_core

    mate = grp(rank, side, 1 - core)
    across = grp(rank, 1 - side, core)

    if fused:
        fills = [
            pltpu.make_async_copy(
                partial_ref.at[:, pl.ds(pl.multiple_of(part * feature_share, feature_share),
                                        feature_share)], own_part, h_local.at[0]),
            pltpu.make_async_copy(residual_ref, own_residual, h_local.at[1])]
        for copy in fills:
            copy.start()

    def w_rows(at_side, at_core):
        return pl.ds(pl.multiple_of((at_side * CORES + at_core) * depth, depth), depth)

    mine = w_rows(side, core)
    locals_ = [pltpu.make_async_copy(wq_ref, wide.at[mine, pl.ds(0, q_cols)], w_local.at[0]),
               pltpu.make_async_copy(wk_ref, wide.at[mine, pl.ds(q_cols, k_cols)], w_local.at[1])]
    for copy in locals_:
        copy.start()

    barrier = pltpu.get_barrier_semaphore()
    for peer in (mate, across):
        pl.semaphore_signal(barrier, inc=1, device_id={"grp": peer}, device_id_type=MESH)
    for d in range(parts):
        for k in range(ranks):
            if d or k:
                pl.semaphore_signal(
                    barrier, inc=1,
                    device_id={"grp": grp(lax.rem(rank + k, ranks), side, core),
                               "tp": lax.rem(part + d, parts)},
                    device_id_type=MESH)
    pl.semaphore_wait(barrier, ranks * parts + 1)

    def p_copy(r, d):
        to = lax.rem(part + d, parts)
        return pltpu.make_async_remote_copy(
            src_ref=partial_ref.at[pl.ds(r * rows, rows),
                                   pl.ds(pl.multiple_of(to * feature_share, feature_share),
                                         feature_share)],
            dst_ref=part_in.at[d - 1, pl.ds(r * rows, rows)],
            send_sem=p_send.at[r, d - 1], recv_sem=p_recv.at[r, d - 1],
            device_id={"tp": to}, device_id_type=MESH)

    if fused:
        for r in range(chunks):
            for d in range(1, parts):
                p_copy(r, d).start()

    def columns(j):
        return pl.ds(pl.multiple_of(j * width, width), width)

    def wx_copy(src, j, to_column):
        return pltpu.make_async_remote_copy(
            src_ref=src.at[:, columns(j)], dst_ref=wide.at[mine, columns(to_column)],
            send_sem=wx_send.at[to_column], recv_sem=wx_recv.at[to_column],
            device_id={"grp": across}, device_id_type=MESH)

    def start_q(j, carry):
        wx_copy(wq_ref, j, j).start()
        return carry

    def start_k(j, carry):
        wx_copy(wk_ref, j, q_steps + j).start()
        return carry

    lax.fori_loop(0, q_steps, start_q, 0)
    lax.fori_loop(0, columns_count - q_steps, start_k, 0)
    m_copies = [pltpu.make_async_remote_copy(
        src_ref=src, dst_ref=dst, send_sem=m_send.at[i], recv_sem=m_recv.at[i],
        device_id={"grp": mate}, device_id_type=MESH)
        for i, (src, dst) in enumerate(((wq_ref, wide.at[mine, pl.ds(0, q_cols)]),
                                        (wk_ref, wide.at[mine, pl.ds(q_cols, k_cols)])))]
    for copy in m_copies:
        copy.start()

    def sum_chunk(r):
        for d in range(1, parts):
            p_copy(r, d).wait_recv()
        here = pl.ds(r * rows, rows)
        block = math.gcd(feature_share, 512)

        def body(c, total):
            at = pl.ds(pl.multiple_of(c * block, block), block)
            value = own_part[here, at].astype(jnp.float32)
            for d in range(1, parts):
                value = value + part_in[d - 1, here, at].astype(jnp.float32)
            value = (own_residual[here, at].astype(jnp.float32) + value).astype(jnp.bfloat16)
            hidden_ref[here, at] = value
            value = value.astype(jnp.float32)
            rows_ref[here, at] = (value * gain_ref[:, at]).astype(jnp.bfloat16)
            value = value * value
            for b in range(block // 128):
                total = total + value[:, b * 128:(b + 1) * 128]
            return total

        total = lax.fori_loop(0, feature_share // block, body, jnp.zeros((rows, 128), jnp.float32))
        square_ref[here, :] = jnp.broadcast_to(
            jnp.sum(total, axis=1, keepdims=True), (rows, 128))

    def piece_at(base, index):
        return pl.ds(pl.multiple_of(base + index * piece, piece), piece)

    def x_ends(r, i, d):
        to = lax.rem(part + d, parts)
        return (rows_ref.at[piece_at(r * rows, to), pl.ds(i * share, share)],
                xs.at[r, piece_at(rank * rows, to)])

    def x_copy(r, i, d):
        src, dst = x_ends(r, i, d)
        return pltpu.make_async_remote_copy(
            src_ref=src, dst_ref=dst, send_sem=x_send.at[r, i, d], recv_sem=x_recv.at[r, rank],
            device_id={"grp": grp(part * held + i, side, core), "tp": lax.rem(part + d, parts)},
            device_id_type=MESH)

    whole_here = rank // held == part

    def x_near(r, i):
        src, dst = x_ends(r, i, 0)
        dst[...] = src[...]

    def each_x(r, far, near):
        for i in range(held):
            here = jnp.logical_and(whole_here, lax.rem(rank, held) == i)
            pl.when(here)(functools.partial(near, r, i))
            pl.when(jnp.logical_not(here))(functools.partial(far, r, i, 0))
            for d in range(1, parts):
                far(r, i, d)

    def x_arrive(r, source):
        at = xs.at[r, piece_at(source * rows, part)]
        pltpu.make_async_remote_copy(
            src_ref=at, dst_ref=at, send_sem=x_send.at[r, 0, 0], recv_sem=x_recv.at[r, source],
            device_id={"grp": mate}, device_id_type=MESH).wait_recv()

    def f_copy(r, source, d):
        at = xs.at[r, piece_at(source * rows, part)]
        return pltpu.make_async_remote_copy(
            src_ref=at, dst_ref=at,
            send_sem=f_send.at[r, source, d - 1], recv_sem=f_recv.at[r, source, d - 1],
            device_id={"tp": lax.rem(part + d, parts)}, device_id_type=MESH)

    def pass_on(r):
        for k in range(ranks):
            source = lax.rem(rank + k, ranks)
            if k:
                x_arrive(r, source)
            else:
                pl.when(jnp.logical_not(whole_here))(functools.partial(x_arrive, r, source))
            for d in range(1, parts):
                f_copy(r, source, d).start()

    def x_wait(r):
        for source in range(ranks):
            for d in range(1, parts):
                at = xs.at[r, piece_at(source * rows, lax.rem(part + parts - d, parts))]
                pltpu.make_async_remote_copy(
                    src_ref=at, dst_ref=at,
                    send_sem=f_send.at[r, source, d - 1], recv_sem=f_recv.at[r, source, d - 1],
                    device_id={"grp": mate}, device_id_type=MESH).wait_recv()

    def q_copy(d):
        return pltpu.make_async_remote_copy(
            src_ref=square_ref, dst_ref=squares.at[d - 1],
            send_sem=q_send.at[d - 1], recv_sem=q_recv.at[d - 1],
            device_id={"tp": lax.rem(part + d, parts)}, device_id_type=MESH)

    if fused:
        for copy in fills:
            copy.wait()
    for r in range(chunks):
        if fused:
            sum_chunk(r)
        each_x(r, lambda r, i, d: x_copy(r, i, d).start(), x_near)
        if r:
            pass_on(r - 1)
    for d in range(1, parts):
        q_copy(d).start()
    pass_on(chunks - 1)

    for copy in locals_:
        copy.wait()
    theirs = w_rows(side, 1 - core)
    for i, (src, dst) in enumerate(((wq_ref, wide.at[theirs, pl.ds(0, q_cols)]),
                                    (wk_ref, wide.at[theirs, pl.ds(q_cols, k_cols)]))):
        pltpu.make_async_remote_copy(
            src_ref=src, dst_ref=dst, send_sem=m_send.at[i], recv_sem=m_recv.at[i],
            device_id={"grp": mate}, device_id_type=MESH).wait_recv()

    mean_square = square_ref[...]
    for d in range(1, parts):
        q_copy(d).wait_recv()
        mean_square = mean_square + squares[d - 1]
    scale_ref[...] = lax.rsqrt(mean_square / (feature_share * parts) + epsilon)

    def wf_copy(j, at_core):
        at = wide.at[w_rows(1 - side, at_core), columns(j)]
        return pltpu.make_async_remote_copy(
            src_ref=at, dst_ref=at, send_sem=wf_send.at[j], recv_sem=wf_recv.at[j],
            device_id={"grp": mate}, device_id_type=MESH)

    def w_arrive(j):
        at = wide.at[w_rows(1 - side, core), columns(j)]
        pltpu.make_async_remote_copy(
            src_ref=at, dst_ref=at, send_sem=wx_send.at[j], recv_sem=wx_recv.at[j],
            device_id={"grp": across}, device_id_type=MESH).wait_recv()
        wf_copy(j, core).start()
        wf_copy(j, 1 - core).wait_recv()

    def place(s):
        first = s < chunks * early
        late = s - chunks * early
        r = jnp.where(first, s // early, lax.rem(late + chunks * early, chunks))
        j = jnp.where(first, lax.rem(s, early), early + late // chunks)
        return r, j

    def multiply(s):
        r, j = place(s)
        pl.when(r == 0)(functools.partial(w_arrive, j))
        for at in range(chunks):
            pl.when(jnp.logical_and(r == at, j == 0))(functools.partial(x_wait, at))
        products[lax.rem(s, slots)] = jnp.dot(
            xs[r], wide[:, columns(j)], preferred_element_type=jnp.float32)

    def chain(out, into, send, recv, s, blocks, to):
        return pltpu.make_async_remote_copy(
            src_ref=out.at[s, pl.ds(0, blocks)], dst_ref=into.at[s, pl.ds(0, blocks)],
            send_sem=send.at[s], recv_sem=recv.at[s],
            device_id={"grp": grp(to, side, core)}, device_id_type=MESH)

    def line(z, going_right, act):
        distance = ranks - 1 - z if going_right else z
        out, into, send, recv = ((right_out, right_in, rt_send, rt_recv) if going_right
                                 else (left_out, left_in, lt_send, lt_recv))
        return functools.partial(act, z, 1 if going_right else -1, distance,
                                 out, into, send, recv)

    def pass_line(z, sign, distance, out, into, send, recv, s):
        ends = ranks - 1 - distance
        slot = lax.rem(s, slots)
        if ends:
            chain(out, into, send, recv, s, distance + 1, z).wait_recv()
        for b in range(distance):
            block = z + sign * (b + 1)
            value = products[slot, pl.ds(block * rows, rows)]
            if ends:
                value = value + into[s, b + 1].astype(jnp.float32)
            out[s, b] = value.astype(jnp.bfloat16)
        if distance:
            chain(out, into, send, recv, s, distance, z + sign).start()

    def drain_line(z, sign, distance, out, into, send, recv, s):
        if distance:
            chain(out, into, send, recv, s, distance, z + sign).wait_send()

    def finish(z, s):
        r, j = place(s)
        slot = lax.rem(s, slots)
        here = pl.ds(pl.multiple_of(r * rows, rows), rows)
        total = products[slot, pl.ds(z * rows, rows)]
        if z:
            total = total + right_in[s, 0].astype(jnp.float32)
        if z < ranks - 1:
            total = total + left_in[s, 0].astype(jnp.float32)
        total = total * scale_ref[here, :][:, :1] + bias_ref[:, columns(j)]
        total = total.astype(jnp.bfloat16)

        def to_query():
            query_ref[here, columns(j)] = total

        def to_keyval():
            keyval_ref[here, columns(j - q_steps)] = total

        pl.when(j < q_steps)(to_query)
        pl.when(j >= q_steps)(to_keyval)

    def step(i, carry):
        pl.when(i < steps)(functools.partial(multiply, i))
        for z in range(ranks):
            def at_rank(z=z):
                for going_right in (True, False):
                    lag = LAG * (z if going_right else ranks - 1 - z)
                    s = i - lag
                    pl.when(jnp.logical_and(s >= 0, s < steps))(
                        functools.partial(line(z, going_right, pass_line), s))
                s = i - LAG * max(z, ranks - 1 - z)
                pl.when(jnp.logical_and(s >= 0, s < steps))(functools.partial(finish, z, s))

            pl.when(rank == z)(at_rank)
        return carry

    lax.fori_loop(0, steps + LAG * (ranks - 1), step, 0)

    if fused:
        for r in range(chunks):
            for d in range(1, parts):
                p_copy(r, d).wait_send()
    for copy in m_copies:
        copy.wait_send()
    for r in range(chunks):
        each_x(r, lambda r, i, d: x_copy(r, i, d).wait_send(), lambda r, i: None)
        for source in range(ranks):
            for d in range(1, parts):
                f_copy(r, source, d).wait_send()
    for d in range(1, parts):
        q_copy(d).wait_send()

    def drain_w(j, carry):
        at = wide.at[mine, columns(j)]
        pltpu.make_async_remote_copy(
            src_ref=at, dst_ref=at, send_sem=wx_send.at[j], recv_sem=wx_recv.at[j],
            device_id={"grp": across}, device_id_type=MESH).wait_send()
        wf_copy(j, core).wait_send()
        return carry

    lax.fori_loop(0, columns_count, drain_w, 0)

    def drain_steps(s, carry):
        for z in range(ranks):
            def at_rank(z=z):
                for going_right in (True, False):
                    line(z, going_right, drain_line)(s)

            pl.when(rank == z)(at_rank)
        return carry

    lax.fori_loop(0, steps, drain_steps, 0)


def project(state, w_query, w_keyval, bias, group, parts, fused):
    if fused:
        count, feature_share = state[1].shape
    else:
        count, feature_share = state[0].shape
    depth, q_cols = w_query.shape
    k_cols = w_keyval.shape[1]
    total = q_cols + k_cols
    width = math.gcd(math.gcd(q_cols, k_cols), 512)
    ranks = group // (CORES * SIDES)
    share = CORES * SIDES * depth
    chunks = min(4, count // (16 * parts))
    rows = count // chunks
    columns_count = total // width
    early = min(3, columns_count)
    steps = chunks * columns_count
    slots = LAG * (ranks - 1) + 1
    held = ranks // parts
    vmem = pl.BlockSpec(memory_space=pltpu.VMEM)
    hbm = pl.BlockSpec(memory_space=pl.ANY)
    dma = pltpu.SemaphoreType.DMA
    bf16 = jnp.bfloat16
    line = pltpu.VMEM((steps, ranks - 1, rows, width), bf16)
    outs = [jax.ShapeDtypeStruct((count, q_cols), bf16),
            jax.ShapeDtypeStruct((count, k_cols), bf16)]
    scratch = []
    if fused:
        outs.insert(0, jax.ShapeDtypeStruct((count, feature_share), bf16))
        scratch = [
            pltpu.VMEM((count, feature_share), bf16),
            pltpu.VMEM((count, feature_share), bf16),
            pltpu.VMEM((parts - 1, count, feature_share), bf16),
            pltpu.VMEM((count, feature_share), bf16),
            pltpu.VMEM((count, 128), jnp.float32),
            dma((2,)), dma((chunks, parts - 1)), dma((chunks, parts - 1)),
        ]
    scratch += [
        pltpu.VMEM((chunks, ranks * rows, share), bf16),
        pltpu.VMEM((share, total), bf16),
        pltpu.VMEM((slots, ranks * rows, width), jnp.float32),
        line, line, line, line,
        pltpu.VMEM((parts - 1, count, 128), jnp.float32),
        pltpu.VMEM((count, 128), jnp.float32),
        dma((2,)), dma((2,)), dma((2,)),
        dma((columns_count,)), dma((columns_count,)),
        dma((columns_count,)), dma((columns_count,)),
        dma((chunks, held, parts)), dma((chunks, ranks)),
        dma((chunks, ranks, parts - 1)), dma((chunks, ranks, parts - 1)),
        dma((parts - 1,)), dma((parts - 1,)),
        dma((steps,)), dma((steps,)), dma((steps,)), dma((steps,)),
    ]
    return pl.pallas_call(
        functools.partial(kernel, ranks, parts, chunks, width, early, fused),
        out_shape=tuple(outs),
        in_specs=([hbm, hbm, vmem] if fused else [vmem, vmem]) + [hbm, hbm, vmem],
        out_specs=(vmem,) * len(outs),
        scratch_shapes=scratch,
        compiler_params=pltpu.CompilerParams(
            collective_id=0, has_side_effects=True, vmem_limit_bytes=62 * 1024 * 1024),
    )(*state, w_query, w_keyval, bias)


def local(group, parts, sections, partials, residual, norm_gain, w_query, w_keyval,
          bias_query, bias_keyval):
    feature_share = residual.shape[2]
    offset = lax.axis_index("tp") * feature_share
    local_gain = lax.dynamic_slice_in_dim(norm_gain, offset, feature_share, 0).astype(jnp.float32)
    bias = jnp.concatenate([bias_query, bias_keyval]).astype(jnp.float32)[None]
    if sections == 1:
        seqs, length = residual.shape[:2]
        count = seqs * length
        hidden, query, keyval = project(
            (partials.reshape(count, -1), residual.reshape(count, -1), local_gain[None]),
            w_query, w_keyval, bias, group, parts, True)
        hidden = hidden.reshape(residual.shape)
    else:
        summed = lax.psum_scatter(
            partials[0], "tp", scatter_dimension=2, tiled=True).astype(jnp.float32)
        hidden = (residual.astype(jnp.float32) + summed).astype(jnp.bfloat16)
        widened = hidden.astype(jnp.float32)
        squares = jnp.sum(widened * widened, axis=-1)
        scaled = (widened * local_gain).astype(jnp.bfloat16)
        scaled = lax.all_gather(scaled, "section", axis=0, tiled=True)
        squares = lax.all_gather(squares, "section", axis=0, tiled=True)
        seqs, length = squares.shape
        count = seqs * length
        squares = jnp.broadcast_to(squares.reshape(-1, 1), (count, 128))
        query, keyval = project(
            (scaled.reshape(count, feature_share), squares), w_query, w_keyval, bias,
            group, parts, False)
    return (hidden, query.reshape(seqs, length, -1), keyval.reshape(seqs, length, -1))


def solution(mesh):
    placed = (
        P("tp", "section", "grp", None),
        P("section", "grp", "tp"),
        P(),
        P("grp", ("section", "tp")),
        P("grp", ("section", "tp")),
        P(("section", "tp")),
        P(("section", "tp")),
    )
    return jax.shard_map(
        functools.partial(local, mesh.shape["grp"], mesh.shape["tp"], mesh.shape["section"]),
        mesh=mesh,
        in_specs=placed,
        out_specs=(
            P("section", "grp", "tp"),
            P(None, "grp", ("section", "tp")),
            P(None, "grp", ("section", "tp")),
        ),
        check_vma=False,
    )
```

time: 233 us -> 181 us (0.78)
  the two profiles are of different devices: /device:TPU:26 before, /device:TPU:0 now
where the time goes in v1:
time: 181 us; the launch traced here: 180 us
  Pallas kernels  171 us (94%)
  local copies, waits for them, and re-layouts  6.72 us (4%)
  other arithmetic  1.93 us (1%)
    pallas_call x1, Pallas kernels, project(): pl.pallas_call(functools.partial(kernel, ranks, parts, chunks, width, ear...  171 us
    unnamed x5, local copies, waits for them, and re-layouts  5.32 us

profile of v1, /device:TPU:0, one launch (start us, length us, event | category | flops | bytes accessed | tf_op | source)
XLA Modules:
  0.0 180.2 jit_solution(155958805618494451)
XLA Ops:
  0.6 0.7 concatenate.15
  1.3 1.3 dynamic-slice_convert_fusion
  2.6 0.7 concatenate.14
  3.3 0.6 maximum_convert_fusion.refs_5_
  4.0 170.9 %shard_map.94 = (bf16[128,4096]{1,0:T(8,128)(2,1)}, bf16[128,4096]{1,0:T(8,128)(2,1)}, bf16[128,1024]{1,0:T(8,128)(2,1)}) custom-call(bf16[128,8192]{1,0:T(8,128)(2,1)} %bitcast.6, bf16[128,4096]{1,0:T(8,128)(2,1)} %bitcast.9, f32[1,4096]{1,0:T(1,128)} %bitcast.11, bf16[512,4096]{1,0:T(8,128)(2,1)} %refs_3_.1, bf16[512,1024]{1,0:T(8,128)(2,1)} %refs_4_.1, ...), custom_call_target="tpu_custom_call" | custom-call | tf_op jit(solution)/shard_map/pallas_call | solution.py:440
  174.8 0.0 copy-start
  174.9 2.3 %copy.13 = bf16[1,128,4096]{2,1,0:T(8,128)(2,1)} copy(bf16[1,128,4096]{2,1,0:T(8,128)(2,1)} %bitcast.8) | data formatting | bytes 2097152
  177.2 2.3 %copy.14 = bf16[1,128,4096]{2,1,0:T(8,128)(2,1)} copy(bf16[1,128,4096]{2,1,0:T(8,128)(2,1)} %bitcast.7) | data formatting | bytes 2097152
  179.5 0.0 copy-done
  179.5 0.7 copy.15
Async XLA Ops:
  174.8 4.6 %copy-start = (bf16[128,1024]{1,0:T(8,128)(2,1)S(1)}, bf16[128,1024]{1,0:T(8,128)(2,1)}, u32[]{:S(2)}) copy-start(bf16[128,1024]{1,0:T(8,128)(2,1)} %get-tuple-element.8) | copy-start | bytes 786436

commit v2 on v1

--- a/solution.py
+++ b/solution.py
@@ -13,6 +13,8 @@
 CORES = 2
 SIDES = 2
 LAG = 2
+EARLY = 2
+EVENTS = (-1.9, 1.5, 2.6, 3.7, 4.75)
 
 
 def kernel(ranks, parts, chunks, width, early, fused, *refs):
@@ -22,18 +24,18 @@
         partial_ref, residual_ref, gain_ref = take(3)
     else:
         given_rows, given_squares = take(2)
-    wq_ref, wk_ref, bias_ref = take(3)
+    wq_ref, wk_ref, bias_q_ref, bias_k_ref = take(4)
     if fused:
         hidden_ref, = take(1)
     query_ref, keyval_ref = take(2)
     if fused:
         own_part, own_residual, part_in, rows_ref, square_ref = take(5)
-        h_local, p_send, p_recv = take(3)
+        gain_row, h_local, p_send, p_recv = take(4)
     else:
         rows_ref, square_ref = given_rows, given_squares
-    (xs, wide, products, right_out, right_in, left_out, left_in, squares, scale_ref,
+    (bias_row, others, xs, wide, products, right_out, right_in, left_out, left_in, squares, scale_ref,
      w_local, m_send, m_recv, wx_send, wx_recv, wf_send, wf_recv,
-     x_send, x_recv, f_send, f_recv, q_send, q_recv,
+     y_send, y_recv, x_send, x_recv, f_send, f_recv, q_send, q_recv,
      rt_send, rt_recv, lt_send, lt_recv) = refs
 
     me = lax.axis_index("grp")
@@ -81,15 +83,20 @@
     barrier = pltpu.get_barrier_semaphore()
     for peer in (mate, across):
         pl.semaphore_signal(barrier, inc=1, device_id={"grp": peer}, device_id_type=MESH)
-    for d in range(parts):
-        for k in range(ranks):
-            if d or k:
-                pl.semaphore_signal(
-                    barrier, inc=1,
-                    device_id={"grp": grp(lax.rem(rank + k, ranks), side, core),
-                               "tp": lax.rem(part + d, parts)},
-                    device_id_type=MESH)
-    pl.semaphore_wait(barrier, ranks * parts + 1)
+    for k in range(1, ranks):
+        pl.semaphore_signal(
+            barrier, inc=1, device_id={"grp": grp(lax.rem(rank + k, ranks), side, core)},
+            device_id_type=MESH)
+    for d in range(1, parts):
+        pl.semaphore_signal(
+            barrier, inc=1, device_id={"tp": lax.rem(part + d, parts)}, device_id_type=MESH)
+    pl.semaphore_wait(barrier, ranks + parts)
+
+    def spread(src, start, length, dst, to):
+        block = math.gcd(length, 1024)
+        for b in range(length // block):
+            value = src[pl.ds(start + b * block, block)].astype(jnp.float32)
+            dst[:, pl.ds(to + b * block, block)] = value.reshape(1, block)
 
     def p_copy(r, d):
         to = lax.rem(part + d, parts)
@@ -101,10 +108,17 @@
             send_sem=p_send.at[r, d - 1], recv_sem=p_recv.at[r, d - 1],
             device_id={"tp": to}, device_id_type=MESH)
 
-    if fused:
-        for r in range(chunks):
-            for d in range(1, parts):
-                p_copy(r, d).start()
+    def send_part(r):
+        for d in range(1, parts):
+            p_copy(r, d).start()
+
+    if fused:
+        for r in range(min(2, chunks)):
+            send_part(r)
+        spread(gain_ref, pl.multiple_of(part * feature_share, feature_share), feature_share,
+               gain_row, 0)
+    spread(bias_q_ref, 0, q_cols, bias_row, 0)
+    spread(bias_k_ref, 0, k_cols, bias_row, q_cols)
 
     def columns(j):
         return pl.ds(pl.multiple_of(j * width, width), width)
@@ -147,7 +161,7 @@
             value = (own_residual[here, at].astype(jnp.float32) + value).astype(jnp.bfloat16)
             hidden_ref[here, at] = value
             value = value.astype(jnp.float32)
-            rows_ref[here, at] = (value * gain_ref[:, at]).astype(jnp.bfloat16)
+            rows_ref[here, at] = (value * gain_row[:, at]).astype(jnp.bfloat16)
             value = value * value
             for b in range(block // 128):
                 total = total + value[:, b * 128:(b + 1) * 128]
@@ -160,37 +174,47 @@
     def piece_at(base, index):
         return pl.ds(pl.multiple_of(base + index * piece, piece), piece)
 
-    def x_ends(r, i, d):
+    def y_copy(r, d):
         to = lax.rem(part + d, parts)
-        return (rows_ref.at[piece_at(r * rows, to), pl.ds(i * share, share)],
-                xs.at[r, piece_at(rank * rows, to)])
-
-    def x_copy(r, i, d):
-        src, dst = x_ends(r, i, d)
-        return pltpu.make_async_remote_copy(
-            src_ref=src, dst_ref=dst, send_sem=x_send.at[r, i, d], recv_sem=x_recv.at[r, rank],
-            device_id={"grp": grp(part * held + i, side, core), "tp": lax.rem(part + d, parts)},
-            device_id_type=MESH)
-
-    whole_here = rank // held == part
-
-    def x_near(r, i):
-        src, dst = x_ends(r, i, 0)
+        return pltpu.make_async_remote_copy(
+            src_ref=rows_ref.at[piece_at(r * rows, to)],
+            dst_ref=others.at[d - 1, pl.ds(r * piece, piece)],
+            send_sem=y_send.at[r, d - 1], recv_sem=y_recv.at[r, d - 1],
+            device_id={"tp": to}, device_id_type=MESH)
+
+    def x_ends(r, d, i):
+        features = pl.ds(i * share, share)
+        src = (others.at[d - 1, pl.ds(r * piece, piece), features] if d
+               else rows_ref.at[piece_at(r * rows, part), features])
+        return src, xs.at[r, piece_at(rank * rows, part)]
+
+    def x_to(d, i):
+        return lax.rem(part + parts - d, parts) * held + i
+
+    def x_copy(r, d, i):
+        src, dst = x_ends(r, d, i)
+        return pltpu.make_async_remote_copy(
+            src_ref=src, dst_ref=dst, send_sem=x_send.at[r, d, i], recv_sem=x_recv.at[r, rank],
+            device_id={"grp": grp(x_to(d, i), side, core)}, device_id_type=MESH)
+
+    def each_x(r, d, far, near):
+        for i in range(held):
+            here = x_to(d, i) == rank
+            if near is not None:
+                pl.when(here)(functools.partial(near, r, d, i))
+            pl.when(jnp.logical_not(here))(functools.partial(far, r, d, i))
+
+    def x_near(r, d, i):
+        src, dst = x_ends(r, d, i)
         dst[...] = src[...]
 
-    def each_x(r, far, near):
-        for i in range(held):
-            here = jnp.logical_and(whole_here, lax.rem(rank, held) == i)
-            pl.when(here)(functools.partial(near, r, i))
-            pl.when(jnp.logical_not(here))(functools.partial(far, r, i, 0))
-            for d in range(1, parts):
-                far(r, i, d)
-
-    def x_arrive(r, source):
-        at = xs.at[r, piece_at(source * rows, part)]
-        pltpu.make_async_remote_copy(
-            src_ref=at, dst_ref=at, send_sem=x_send.at[r, 0, 0], recv_sem=x_recv.at[r, source],
-            device_id={"grp": mate}, device_id_type=MESH).wait_recv()
+    def x_start(r, d):
+        each_x(r, d, lambda r, d, i: x_copy(r, d, i).start(), x_near)
+
+    def relay(r):
+        for d in range(1, parts):
+            y_copy(r, d).wait_recv()
+            x_start(r, d)
 
     def f_copy(r, source, d):
         at = xs.at[r, piece_at(source * rows, part)]
@@ -203,9 +227,11 @@
         for k in range(ranks):
             source = lax.rem(rank + k, ranks)
             if k:
-                x_arrive(r, source)
-            else:
-                pl.when(jnp.logical_not(whole_here))(functools.partial(x_arrive, r, source))
+                at = xs.at[r, piece_at(source * rows, part)]
+                pltpu.make_async_remote_copy(
+                    src_ref=at, dst_ref=at, send_sem=x_send.at[r, 0, 0],
+                    recv_sem=x_recv.at[r, source],
+                    device_id={"grp": mate}, device_id_type=MESH).wait_recv()
             for d in range(1, parts):
                 f_copy(r, source, d).start()
 
@@ -218,39 +244,33 @@
                     send_sem=f_send.at[r, source, d - 1], recv_sem=f_recv.at[r, source, d - 1],
                     device_id={"grp": mate}, device_id_type=MESH).wait_recv()
 
-    def q_copy(d):
-        return pltpu.make_async_remote_copy(
-            src_ref=square_ref, dst_ref=squares.at[d - 1],
-            send_sem=q_send.at[d - 1], recv_sem=q_recv.at[d - 1],
+    def q_copy(r, d):
+        here = pl.ds(r * rows, rows)
+        return pltpu.make_async_remote_copy(
+            src_ref=square_ref.at[here], dst_ref=squares.at[d - 1, here],
+            send_sem=q_send.at[r, d - 1], recv_sem=q_recv.at[r, d - 1],
             device_id={"tp": lax.rem(part + d, parts)}, device_id_type=MESH)
+
+    def prepare(r):
+        if fused:
+            sum_chunk(r)
+        for d in range(1, parts):
+            y_copy(r, d).start()
+        x_start(r, 0)
+        for d in range(1, parts):
+            q_copy(r, d).start()
 
     if fused:
         for copy in fills:
             copy.wait()
-    for r in range(chunks):
-        if fused:
-            sum_chunk(r)
-        each_x(r, lambda r, i, d: x_copy(r, i, d).start(), x_near)
-        if r:
-            pass_on(r - 1)
-    for d in range(1, parts):
-        q_copy(d).start()
-    pass_on(chunks - 1)
-
-    for copy in locals_:
-        copy.wait()
-    theirs = w_rows(side, 1 - core)
-    for i, (src, dst) in enumerate(((wq_ref, wide.at[theirs, pl.ds(0, q_cols)]),
-                                    (wk_ref, wide.at[theirs, pl.ds(q_cols, k_cols)]))):
-        pltpu.make_async_remote_copy(
-            src_ref=src, dst_ref=dst, send_sem=m_send.at[i], recv_sem=m_recv.at[i],
-            device_id={"grp": mate}, device_id_type=MESH).wait_recv()
-
-    mean_square = square_ref[...]
-    for d in range(1, parts):
-        q_copy(d).wait_recv()
-        mean_square = mean_square + squares[d - 1]
-    scale_ref[...] = lax.rsqrt(mean_square / (feature_share * parts) + epsilon)
+
+    def set_scale(r):
+        here = pl.ds(r * rows, rows)
+        mean_square = square_ref[here]
+        for d in range(1, parts):
+            q_copy(r, d).wait_recv()
+            mean_square = mean_square + squares[d - 1, here]
+        scale_ref[here] = lax.rsqrt(mean_square / (feature_share * parts) + epsilon)
 
     def wf_copy(j, at_core):
         at = wide.at[w_rows(1 - side, at_core), columns(j)]
@@ -266,18 +286,31 @@
         wf_copy(j, core).start()
         wf_copy(j, 1 - core).wait_recv()
 
+    runs = []
+    for r in range(chunks):
+        before = min(columns_count, early + min(r - 1, 1)) if r else 0
+        after = columns_count if r == chunks - 1 else min(columns_count, early + min(r, 1))
+        if before:
+            runs.append((r, 1, 0, before))
+        if after > before:
+            runs.append((0, r + 1, before, after))
+    ends = [0]
+    segments = [0] * chunks
+    for r0, nr, j0, j1 in runs:
+        ends.append(ends[-1] + nr * (j1 - j0))
+        segments[r0 + nr - 1] = ends[-1]
+
     def place(s):
-        first = s < chunks * early
-        late = s - chunks * early
-        r = jnp.where(first, s // early, lax.rem(late + chunks * early, chunks))
-        j = jnp.where(first, lax.rem(s, early), early + late // chunks)
+        r, j = s, s
+        for (r0, nr, j0, _), begin in zip(runs, ends):
+            inside = s >= begin
+            r = jnp.where(inside, r0 + lax.rem(s - begin, nr), r)
+            j = jnp.where(inside, j0 + (s - begin) // nr, j)
         return r, j
 
     def multiply(s):
         r, j = place(s)
         pl.when(r == 0)(functools.partial(w_arrive, j))
-        for at in range(chunks):
-            pl.when(jnp.logical_and(r == at, j == 0))(functools.partial(x_wait, at))
         products[lax.rem(s, slots)] = jnp.dot(
             xs[r], wide[:, columns(j)], preferred_element_type=jnp.float32)
 
@@ -321,7 +354,7 @@
             total = total + right_in[s, 0].astype(jnp.float32)
         if z < ranks - 1:
             total = total + left_in[s, 0].astype(jnp.float32)
-        total = total * scale_ref[here, :][:, :1] + bias_ref[:, columns(j)]
+        total = total * scale_ref[here, :][:, :1] + bias_row[:, columns(j)]
         total = total.astype(jnp.bfloat16)
 
         def to_query():
@@ -348,7 +381,33 @@
             pl.when(rank == z)(at_rank)
         return carry
 
-    lax.fori_loop(0, steps + LAG * (ranks - 1), step, 0)
+    def load_own():
+        for copy in locals_:
+            copy.wait()
+        theirs = w_rows(side, 1 - core)
+        for i, (src, dst) in enumerate(((wq_ref, wide.at[theirs, pl.ds(0, q_cols)]),
+                                        (wk_ref, wide.at[theirs, pl.ds(q_cols, k_cols)]))):
+            pltpu.make_async_remote_copy(
+                src_ref=src, dst_ref=dst, send_sem=m_send.at[i], recv_sem=m_recv.at[i],
+                device_id={"grp": mate}, device_id_type=MESH).wait_recv()
+
+    def segment(r):
+        if r == 0:
+            load_own()
+        x_wait(r)
+        set_scale(r)
+        lax.fori_loop(segments[r - 1] if r else 0,
+                      segments[r] + (LAG * (ranks - 1) if r == chunks - 1 else 0), step, 0)
+
+    at = EVENTS
+    events = []
+    for r in range(chunks):
+        events += [(r, prepare, r), (r + at[1], relay, r), (r + at[2], pass_on, r),
+                   (r + (at[4] if r else at[3]), segment, r)]
+        if fused and r > 1:
+            events.append((r + at[0], send_part, r))
+    for _, event, r in sorted(events, key=lambda e: e[0]):
+        event(r)
 
     if fused:
         for r in range(chunks):
@@ -357,12 +416,14 @@
     for copy in m_copies:
         copy.wait_send()
     for r in range(chunks):
-        each_x(r, lambda r, i, d: x_copy(r, i, d).wait_send(), lambda r, i: None)
-        for source in range(ranks):
-            for d in range(1, parts):
+        for d in range(parts):
+            each_x(r, d, lambda r, d, i: x_copy(r, d, i).wait_send(), None)
+        for d in range(1, parts):
+            y_copy(r, d).wait_send()
+            for source in range(ranks):
                 f_copy(r, source, d).wait_send()
-    for d in range(1, parts):
-        q_copy(d).wait_send()
+        for d in range(1, parts):
+            q_copy(r, d).wait_send()
 
     def drain_w(j, carry):
         at = wide.at[mine, columns(j)]
@@ -386,7 +447,7 @@
     lax.fori_loop(0, steps, drain_steps, 0)
 
 
-def project(state, w_query, w_keyval, bias, group, parts, fused):
+def project(state, w_query, w_keyval, biases, group, parts, fused):
     if fused:
         count, feature_share = state[1].shape
     else:
@@ -400,7 +461,7 @@
     chunks = min(4, count // (16 * parts))
     rows = count // chunks
     columns_count = total // width
-    early = min(3, columns_count)
+    early = min(EARLY, columns_count)
     steps = chunks * columns_count
     slots = LAG * (ranks - 1) + 1
     held = ranks // parts
@@ -420,9 +481,12 @@
             pltpu.VMEM((parts - 1, count, feature_share), bf16),
             pltpu.VMEM((count, feature_share), bf16),
             pltpu.VMEM((count, 128), jnp.float32),
+            pltpu.VMEM((1, feature_share), jnp.float32),
             dma((2,)), dma((chunks, parts - 1)), dma((chunks, parts - 1)),
         ]
     scratch += [
+        pltpu.VMEM((1, total), jnp.float32),
+        pltpu.VMEM((parts - 1, count // parts, feature_share), bf16),
         pltpu.VMEM((chunks, ranks * rows, share), bf16),
         pltpu.VMEM((share, total), bf16),
         pltpu.VMEM((slots, ranks * rows, width), jnp.float32),
@@ -432,36 +496,74 @@
         dma((2,)), dma((2,)), dma((2,)),
         dma((columns_count,)), dma((columns_count,)),
         dma((columns_count,)), dma((columns_count,)),
-        dma((chunks, held, parts)), dma((chunks, ranks)),
+        dma((chunks, parts - 1)), dma((chunks, parts - 1)),
+        dma((chunks, parts, held)), dma((chunks, ranks)),
         dma((chunks, ranks, parts - 1)), dma((chunks, ranks, parts - 1)),
-        dma((parts - 1,)), dma((parts - 1,)),
+        dma((chunks, parts - 1)), dma((chunks, parts - 1)),
         dma((steps,)), dma((steps,)), dma((steps,)), dma((steps,)),
     ]
     return pl.pallas_call(
         functools.partial(kernel, ranks, parts, chunks, width, early, fused),
         out_shape=tuple(outs),
-        in_specs=([hbm, hbm, vmem] if fused else [vmem, vmem]) + [hbm, hbm, vmem],
+        in_specs=([hbm, hbm, vmem] if fused else [vmem, vmem]) + [hbm, hbm, vmem, vmem],
         out_specs=(vmem,) * len(outs),
         scratch_shapes=scratch,
         compiler_params=pltpu.CompilerParams(
             collective_id=0, has_side_effects=True, vmem_limit_bytes=62 * 1024 * 1024),
-    )(*state, w_query, w_keyval, bias)
+    )(*state, w_query, w_keyval, *biases)
+
+
+def hand_over(cuts, *refs):
+    count = len(cuts)
+    sources, targets = refs[:count], refs[count:2 * count]
+    buffers, taken, given = refs[2 * count:3 * count], refs[-2], refs[-1]
+
+    def copies(i, c):
+        rows = sources[i].shape[0] // cuts[i]
+        here = pl.ds(c * rows, rows)
+        return (pltpu.make_async_copy(sources[i].at[here], buffers[i].at[here], taken.at[i, c]),
+                pltpu.make_async_copy(buffers[i].at[here], targets[i].at[here], given.at[i, c]))
+
+    every = [copies(i, c) for i in range(count) for c in range(cuts[i])]
+    for copy, _ in every:
+        copy.start()
+    for copy, onward in every:
+        copy.wait()
+        onward.start()
+    for _, onward in every:
+        onward.wait()
+
+
+def place(*arrays):
+    cuts = [4 if a.shape[0] * a.shape[1] > 2 ** 18 and a.shape[0] % 64 == 0 else 1 for a in arrays]
+    anywhere = pl.BlockSpec(memory_space=pl.ANY)
+    dma = pltpu.SemaphoreType.DMA
+    return pl.pallas_call(
+        functools.partial(hand_over, cuts),
+        out_shape=tuple(jax.ShapeDtypeStruct(a.shape, a.dtype) for a in arrays),
+        in_specs=[anywhere] * len(arrays),
+        out_specs=(anywhere,) * len(arrays),
+        scratch_shapes=[pltpu.VMEM(a.shape, a.dtype) for a in arrays] + [
+            dma((len(arrays), max(cuts))), dma((len(arrays), max(cuts)))],
+    )(*arrays)
 
 
 def local(group, parts, sections, partials, residual, norm_gain, w_query, w_keyval,
           bias_query, bias_keyval):
     feature_share = residual.shape[2]
-    offset = lax.axis_index("tp") * feature_share
-    local_gain = lax.dynamic_slice_in_dim(norm_gain, offset, feature_share, 0).astype(jnp.float32)
-    bias = jnp.concatenate([bias_query, bias_keyval]).astype(jnp.float32)[None]
+    biases = (bias_query, bias_keyval)
     if sections == 1:
         seqs, length = residual.shape[:2]
         count = seqs * length
         hidden, query, keyval = project(
-            (partials.reshape(count, -1), residual.reshape(count, -1), local_gain[None]),
-            w_query, w_keyval, bias, group, parts, True)
+            (partials.reshape(count, -1), residual.reshape(count, -1), norm_gain),
+            w_query, w_keyval, biases, group, parts, True)
+        hidden, query, keyval = place(hidden, query, keyval)
         hidden = hidden.reshape(residual.shape)
     else:
+        offset = lax.axis_index("tp") * feature_share
+        local_gain = lax.dynamic_slice_in_dim(
+            norm_gain, offset, feature_share, 0).astype(jnp.float32)
         summed = lax.psum_scatter(
             partials[0], "tp", scatter_dimension=2, tiled=True).astype(jnp.float32)
         hidden = (residual.astype(jnp.float32) + summed).astype(jnp.bfloat16)
@@ -474,7 +576,7 @@
         count = seqs * length
         squares = jnp.broadcast_to(squares.reshape(-1, 1), (count, 128))
         query, keyval = project(
-            (scaled.reshape(count, feature_share), squares), w_query, w_keyval, bias,
+            (scaled.reshape(count, feature_share), squares), w_query, w_keyval, biases,
             group, parts, False)
     return (hidden, query.reshape(seqs, length, -1), keyval.reshape(seqs, length, -1))
 

time: 181 us -> 155 us (0.86)
  Pallas kernels: 171 us -> 154 us
  local copies, waits for them, and re-layouts: 6.72 us -> 0 us
  other arithmetic: 1.93 us -> 0 us
    pallas_call x1, Pallas kernels: 171 us -> 151 us  [project(): pl.pallas_call(functools.partial(kernel, ranks, parts, chunks, width, ear...]
    unnamed x5 -> x0, local copies, waits for them, and re-layouts: 5.32 us -> none
    pallas_call x0 -> x1, Pallas kernels: none -> 2.55 us  [place(): pl.pallas_call(functools.partial(hand_over, cuts), out_shape=tuple((jax.S...]
where the time goes in v2:
time: 155 us
  Pallas kernels  154 us (99%)
    pallas_call x1, Pallas kernels, project(): pl.pallas_call(functools.partial(kernel, ranks, parts, chunks, width, ear...  151 us

profile of v2, /device:TPU:0, one launch (start us, length us, event | category | flops | bytes accessed | tf_op | source)
XLA Modules:
  0.0 154.5 jit_solution(7869215485053968207)
XLA Ops:
  0.6 151.3 %shard_map.94 = (bf16[128,4096]{1,0:T(8,128)(2,1)}, bf16[128,4096]{1,0:T(8,128)(2,1)}, bf16[128,1024]{1,0:T(8,128)(2,1)}) custom-call(bf16[128,8192]{1,0:T(8,128)(2,1)} %bitcast.5, bf16[128,4096]{1,0:T(8,128)(2,1)} %bitcast.6, bf16[8192]{0:T(1024)(128)(2,1)} %refs_2_.1, bf16[512,4096]{1,0:T(8,128)(2,1)} %refs_3_.1, bf16[512,1024]{1,0:T(8,128)(2,1)} %refs_4_.1, ...), custom_call_target="tpu_custom_call" | custom-call | tf_op jit(solution)/shard_map/pallas_call | solution.py:505
  152.0 2.6 %shard_map.95 = (bf16[128,4096]{1,0:T(8,128)(2,1)}, bf16[128,4096]{1,0:T(8,128)(2,1)}, bf16[128,1024]{1,0:T(8,128)(2,1)}) custom-call(bf16[128,4096]{1,0:T(8,128)(2,1)} %get-tuple-element.9.refs_0_, bf16[128,4096]{1,0:T(8,128)(2,1)} %get-tuple-element.10.refs_1_, bf16[128,1024]{1,0:T(8,128)(2,1)} %get-tuple-element.11.refs_2_), custom_call_target="tpu_custom_call" | custom-call | tf_op jit(solution)/shard_map/pallas_call | solution.py:541

commit v3 on v2

--- a/solution.py
+++ b/solution.py
@@ -14,7 +14,6 @@
 SIDES = 2
 LAG = 2
 EARLY = 2
-EVENTS = (-1.9, 1.5, 2.6, 3.7, 4.75)
 
 
 def kernel(ranks, parts, chunks, width, early, fused, *refs):
@@ -399,13 +398,12 @@
         lax.fori_loop(segments[r - 1] if r else 0,
                       segments[r] + (LAG * (ranks - 1) if r == chunks - 1 else 0), step, 0)
 
-    at = EVENTS
     events = []
     for r in range(chunks):
-        events += [(r, prepare, r), (r + at[1], relay, r), (r + at[2], pass_on, r),
-                   (r + (at[4] if r else at[3]), segment, r)]
+        events += [(r, prepare, r), (r + 1.5, relay, r), (r + 2.6, pass_on, r),
+                   (r + (4.55 if r else 3.7), segment, r)]
         if fused and r > 1:
-            events.append((r + at[0], send_part, r))
+            events.append((r - 1.9, send_part, r))
     for _, event, r in sorted(events, key=lambda e: e[0]):
         event(r)
 

time: 155 us -> 151 us (0.974)
  Pallas kernels: 154 us -> 150 us
    pallas_call x1, Pallas kernels: 151 us -> 147 us  [project(): pl.pallas_call(functools.partial(kernel, ranks, parts, chunks, width, ear...]
where the time goes in v3:
time: 151 us
  Pallas kernels  150 us (99%)
    pallas_call x1, Pallas kernels, project(): pl.pallas_call(functools.partial(kernel, ranks, parts, chunks, width, ear...  147 us

profile of v3, /device:TPU:0, one launch (start us, length us, event | category | flops | bytes accessed | tf_op | source)
XLA Modules:
  0.0 150.6 jit_solution(7420592173612156461)
XLA Ops:
  0.6 147.4 %shard_map.94 = (bf16[128,4096]{1,0:T(8,128)(2,1)}, bf16[128,4096]{1,0:T(8,128)(2,1)}, bf16[128,1024]{1,0:T(8,128)(2,1)}) custom-call(bf16[128,8192]{1,0:T(8,128)(2,1)} %bitcast.5, bf16[128,4096]{1,0:T(8,128)(2,1)} %bitcast.6, bf16[8192]{0:T(1024)(128)(2,1)} %refs_2_.1, bf16[512,4096]{1,0:T(8,128)(2,1)} %refs_3_.1, bf16[512,1024]{1,0:T(8,128)(2,1)} %refs_4_.1, ...), custom_call_target="tpu_custom_call" | custom-call | tf_op jit(solution)/shard_map/pallas_call | solution.py:503
  148.1 2.6 %shard_map.95 = (bf16[128,4096]{1,0:T(8,128)(2,1)}, bf16[128,4096]{1,0:T(8,128)(2,1)}, bf16[128,1024]{1,0:T(8,128)(2,1)}) custom-call(bf16[128,4096]{1,0:T(8,128)(2,1)} %get-tuple-element.9.refs_0_, bf16[128,4096]{1,0:T(8,128)(2,1)} %get-tuple-element.10.refs_1_, bf16[128,1024]{1,0:T(8,128)(2,1)} %get-tuple-element.11.refs_2_), custom_call_target="tpu_custom_call" | custom-call | tf_op jit(solution)/shard_map/pallas_call | solution.py:539

commit v4 on v3

--- a/solution.py
+++ b/solution.py
@@ -12,8 +12,8 @@
 MESH = pl.DeviceIdType.MESH
 CORES = 2
 SIDES = 2
-LAG = 2
-EARLY = 2
+LAG = 3
+EARLY = 3
 
 
 def kernel(ranks, parts, chunks, width, early, fused, *refs):
@@ -277,12 +277,15 @@
             src_ref=at, dst_ref=at, send_sem=wf_send.at[j], recv_sem=wf_recv.at[j],
             device_id={"grp": mate}, device_id_type=MESH)
 
-    def w_arrive(j):
+    def w_forward(j):
         at = wide.at[w_rows(1 - side, core), columns(j)]
         pltpu.make_async_remote_copy(
             src_ref=at, dst_ref=at, send_sem=wx_send.at[j], recv_sem=wx_recv.at[j],
             device_id={"grp": across}, device_id_type=MESH).wait_recv()
         wf_copy(j, core).start()
+
+    def w_arrive(j):
+        pl.when(j >= early)(functools.partial(w_forward, j))
         wf_copy(j, 1 - core).wait_recv()
 
     runs = []
@@ -313,10 +316,11 @@
         products[lax.rem(s, slots)] = jnp.dot(
             xs[r], wide[:, columns(j)], preferred_element_type=jnp.float32)
 
-    def chain(out, into, send, recv, s, blocks, to):
-        return pltpu.make_async_remote_copy(
-            src_ref=out.at[s, pl.ds(0, blocks)], dst_ref=into.at[s, pl.ds(0, blocks)],
-            send_sem=send.at[s], recv_sem=recv.at[s],
+    def chain(out, into, send, recv, s, distance, far, to):
+        blocks = pl.ds(distance - 1, 1) if far else pl.ds(0, distance - 1)
+        return pltpu.make_async_remote_copy(
+            src_ref=out.at[s, blocks], dst_ref=into.at[s, blocks],
+            send_sem=send.at[s, int(far)], recv_sem=recv.at[s, int(far)],
             device_id={"grp": grp(to, side, core)}, device_id_type=MESH)
 
     def line(z, going_right, act):
@@ -329,20 +333,22 @@
     def pass_line(z, sign, distance, out, into, send, recv, s):
         ends = ranks - 1 - distance
         slot = lax.rem(s, slots)
-        if ends:
-            chain(out, into, send, recv, s, distance + 1, z).wait_recv()
-        for b in range(distance):
-            block = z + sign * (b + 1)
-            value = products[slot, pl.ds(block * rows, rows)]
-            if ends:
-                value = value + into[s, b + 1].astype(jnp.float32)
-            out[s, b] = value.astype(jnp.bfloat16)
-        if distance:
-            chain(out, into, send, recv, s, distance, z + sign).start()
+        for far in (True, False):
+            if ends and (far or distance):
+                chain(out, into, send, recv, s, distance + 1, far, z).wait_recv()
+            for b in range(max(distance - 1, 0), distance) if far else range(distance - 1):
+                block = z + sign * (b + 1)
+                value = products[slot, pl.ds(block * rows, rows)]
+                if ends:
+                    value = value + into[s, b + 1].astype(jnp.float32)
+                out[s, b] = value.astype(jnp.bfloat16)
+            if distance > (0 if far else 1):
+                chain(out, into, send, recv, s, distance, far, z + sign).start()
 
     def drain_line(z, sign, distance, out, into, send, recv, s):
-        if distance:
-            chain(out, into, send, recv, s, distance, z + sign).wait_send()
+        for far in (True, False):
+            if distance > (0 if far else 1):
+                chain(out, into, send, recv, s, distance, far, z + sign).wait_send()
 
     def finish(z, s):
         r, j = place(s)
@@ -393,6 +399,8 @@
     def segment(r):
         if r == 0:
             load_own()
+            for j in range(early):
+                w_forward(j)
         x_wait(r)
         set_scale(r)
         lax.fori_loop(segments[r - 1] if r else 0,
@@ -498,7 +506,7 @@
         dma((chunks, parts, held)), dma((chunks, ranks)),
         dma((chunks, ranks, parts - 1)), dma((chunks, ranks, parts - 1)),
         dma((chunks, parts - 1)), dma((chunks, parts - 1)),
-        dma((steps,)), dma((steps,)), dma((steps,)), dma((steps,)),
+        dma((steps, 2)), dma((steps, 2)), dma((steps, 2)), dma((steps, 2)),
     ]
     return pl.pallas_call(
         functools.partial(kernel, ranks, parts, chunks, width, early, fused),

time: 151 us -> 148 us (0.980)
  Pallas kernels: 150 us -> 147 us
    pallas_call x1, Pallas kernels: 147 us -> 145 us  [project(): pl.pallas_call(functools.partial(kernel, ranks, parts, chunks, width, ear...]
where the time goes in v4:
time: 148 us
  Pallas kernels  147 us (99%)
    pallas_call x1, Pallas kernels, project(): pl.pallas_call(functools.partial(kernel, ranks, parts, chunks, width, ear...  145 us

profile of v4, /device:TPU:0, one launch (start us, length us, event | category | flops | bytes accessed | tf_op | source)
XLA Modules:
  0.0 148.0 jit_solution(15032966032906643533)
XLA Ops:
  0.6 144.8 %shard_map.94 = (bf16[128,4096]{1,0:T(8,128)(2,1)}, bf16[128,4096]{1,0:T(8,128)(2,1)}, bf16[128,1024]{1,0:T(8,128)(2,1)}) custom-call(bf16[128,8192]{1,0:T(8,128)(2,1)} %bitcast.5, bf16[128,4096]{1,0:T(8,128)(2,1)} %bitcast.6, bf16[8192]{0:T(1024)(128)(2,1)} %refs_2_.1, bf16[512,4096]{1,0:T(8,128)(2,1)} %refs_3_.1, bf16[512,1024]{1,0:T(8,128)(2,1)} %refs_4_.1, ...), custom_call_target="tpu_custom_call" | custom-call | tf_op jit(solution)/shard_map/pallas_call | solution.py:511
  145.4 2.6 %shard_map.95 = (bf16[128,4096]{1,0:T(8,128)(2,1)}, bf16[128,4096]{1,0:T(8,128)(2,1)}, bf16[128,1024]{1,0:T(8,128)(2,1)}) custom-call(bf16[128,4096]{1,0:T(8,128)(2,1)} %get-tuple-element.9.refs_0_, bf16[128,4096]{1,0:T(8,128)(2,1)} %get-tuple-element.10.refs_1_, bf16[128,1024]{1,0:T(8,128)(2,1)} %get-tuple-element.11.refs_2_), custom_call_target="tpu_custom_call" | custom-call | tf_op jit(solution)/shard_map/pallas_call | solution.py:547
